TPU v7x, 32 devices: a whole 2x2x4 slice. The times are simulated.
32 devices in a mesh: tm: 8 (over y, x, core), batch: 4 (over z).
Axes of the slice: x: 2, y: 2, z: 4, core: 2. Of those that a mesh axis runs over, the one named last changes fastest.
Arguments:
- hidden_states: bfloat16 [4, 1024, 5120], P('batch', 'tm'), may hold values from -6 to 6
- gen_weight: bfloat16 [64, 5120], replicated, may hold values from -0.078125 to 0.078125
- noise_field: bfloat16 [4, 64, 1024], P('batch', None, 'tm'), may hold values from -6 to 6
- timesteps: int32 [4], P('batch'), may hold values from 200 to 999
- embed_real: bfloat16 [128, 5120], replicated, may hold values from -0.5 to 0.5
- time_real: bfloat16 [256, 3, 5120], P('tm'), may hold values from -0.375 to 0.375
- query_real: bfloat16 [5120, 1024], P(None, 'tm'), may hold values from -3 to 3
- key_real: bfloat16 [5120, 1024], P(None, 'tm'), may hold values from -3 to 3
- value_real: bfloat16 [5120, 1024], P(None, 'tm'), may hold values from -0.078125 to 0.078125
- out_real: bfloat16 [1024, 5120], P('tm'), may hold values from -0.1875 to 0.1875
- gain_real: float32 [2, 1024], P(None, 'tm'), may hold values from 0.25 to 3
- proj_real: bfloat16 [64, 5120], replicated, may hold values from -0.078125 to 0.078125
- embed_fake: bfloat16 [128, 5120], replicated, may hold values from -0.5 to 0.5
- time_fake: bfloat16 [256, 3, 5120], P('tm'), may hold values from -0.375 to 0.375
- query_fake: bfloat16 [5120, 1024], P(None, 'tm'), may hold values from -3 to 3
- key_fake: bfloat16 [5120, 1024], P(None, 'tm'), may hold values from -3 to 3
- value_fake: bfloat16 [5120, 1024], P(None, 'tm'), may hold values from -0.078125 to 0.078125
- out_fake: bfloat16 [1024, 5120], P('tm'), may hold values from -0.1875 to 0.1875
- gain_fake: float32 [2, 1024], P(None, 'tm'), may hold values from 0.25 to 3
- proj_fake: bfloat16 [64, 5120], replicated, may hold values from -0.078125 to 0.078125
Outputs:
- dmd_gradient: float32 [4, 64, 1024], P('batch', None, 'tm')
- weight_grad: float32 [64, 5120], replicated
All inputs are finite; a program needn't handle non-finite values.
Results may differ from a plain program's by a relative error of at most 0.019.
Values may be sent and summed in bfloat16 or wider, within the bound.
A program may use at most 128 MiB of HBM per device.

v0:
```python
import math
import jax
import jax.numpy as jnp
from jax import lax
from jax.sharding import PartitionSpec as P

HD = 128
FREQ = 256
FTOK = 128
norm_floor = 0.05
gap_floor = 0.25
highest = lax.Precision.HIGHEST


def from_behind(shard, axis, by):
    size = lax.axis_size(axis)
    pairs = [(i, i + by) for i in range(size) if 0 <= i + by < size]
    return lax.ppermute(shard, axis, pairs)


def sinusoid(time_step):
    half_freq = FREQ // 2
    frequency = jnp.exp(-math.log(10000.0) * jnp.arange(half_freq, dtype=jnp.float32) / half_freq)
    angles = time_step.astype(jnp.float32) * frequency
    return jnp.concatenate([jnp.cos(angles), jnp.sin(angles)]).astype(jnp.bfloat16)


def embed_stats(stacked, embed_table):
    embedded = lax.dot_general(
        stacked, embed_table, (((0,), (0,)), ((), ())), preferred_element_type=jnp.float32
    )
    row_mean = jnp.mean(embedded, axis=1)
    centered = embedded - row_mean[:, None]
    rscale = lax.rsqrt(jnp.mean(centered * centered, axis=1) + norm_floor)
    return (embedded, row_mean, rscale)


def fold_heads(embed_table, modulation, query_proj, key_proj, value_proj):
    scale_row = 1.0 + modulation[1]
    widened = embed_table.astype(jnp.float32) * scale_row[None, :]

    def fold_one(weight):
        wide_weight = weight.astype(jnp.float32)
        main_part = jnp.dot(widened, wide_weight, precision=highest)
        column_sum = jnp.dot(scale_row, wide_weight, precision=highest)
        offset = jnp.dot(modulation[0], wide_weight, precision=highest)
        return jnp.concatenate([main_part, column_sum[None, :], offset[None, :]], axis=0)

    return jnp.stack([fold_one(query_proj), fold_one(key_proj), fold_one(value_proj)])


def project(stacked, row_mean, rscale, folded):
    kin_rows = stacked.shape[0]
    base_part = jnp.einsum(
        "kr,pkc->prc", stacked.astype(jnp.float32), folded[:, :kin_rows], precision=highest
    )
    return (
        rscale[None, :, None] * base_part
        - (rscale * row_mean)[None, :, None] * folded[:, kin_rows][:, None, :]
        + folded[:, kin_rows + 1][:, None, :]
    )


def rms_round(vector, total_sq, columns, gain_row):
    return (
        vector * lax.rsqrt(total_sq / columns + norm_floor)[:, None] * gain_row[None, :]
    ).astype(jnp.bfloat16)


def attend(query_norm, key_norm, value_norm):
    token_count = query_norm.shape[0]
    block_rows = min(512, token_count)
    frames = jnp.arange(token_count, dtype=jnp.int32) // FTOK

    def one_block(row_start):
        query_block = lax.dynamic_slice_in_dim(query_norm, row_start, block_rows, 0)
        scores = jnp.einsum(
            "qhd,khd->hqk", query_block, key_norm, preferred_element_type=jnp.float32
        ) / math.sqrt(HD)
        query_frames = lax.dynamic_slice_in_dim(frames, row_start, block_rows, 0)
        allowed = frames[None, :] <= query_frames[:, None]
        scores = jnp.where(allowed[None], scores, -1e30)
        row_peak = jnp.max(scores, axis=2, keepdims=True)
        exp_scores = jnp.exp(scores - row_peak)
        attn_probs = (exp_scores / jnp.sum(exp_scores, axis=2, keepdims=True)).astype(jnp.bfloat16)
        return jnp.einsum(
            "hqk,khd->qhd", attn_probs, value_norm, preferred_element_type=jnp.float32
        ).astype(jnp.bfloat16)

    starts = jnp.arange(token_count // block_rows, dtype=jnp.int32) * block_rows
    pieces = lax.map(one_block, starts)
    return pieces.reshape(token_count, query_norm.shape[1], query_norm.shape[2])


def head_terms(attended, out_rows, modulation, final_proj):
    gated = out_rows.astype(jnp.float32) * modulation[2][None, :]
    folded_out = lax.dot_general(
        gated, final_proj.astype(jnp.float32), (((1,), (1,)), ((), ())), precision=highest
    )
    flat_heads = attended.reshape(attended.shape[0], -1).astype(jnp.float32)
    return lax.dot_general(folded_out, flat_heads, (((0,), (1,)), ((), ())), precision=highest)


def per_device(
    hidden_states,
    gen_weight,
    noise_field,
    timesteps,
    embed_real,
    time_real,
    query_real,
    key_real,
    value_real,
    out_real,
    gain_real,
    proj_real,
    embed_fake,
    time_fake,
    query_fake,
    key_fake,
    value_fake,
    out_fake,
    gain_fake,
    proj_fake,
):
    devices = lax.axis_size("tm")
    frame_tokens = hidden_states.shape[1]
    tokens = frame_tokens * devices
    patch_rows = gen_weight.shape[0]
    time_step = timesteps[0]
    level_raw = time_step.astype(jnp.float32) / 1000.0
    noise_level = 5.0 * level_raw / (1.0 + 4.0 * level_raw)
    generated = lax.dot_general(
        gen_weight, hidden_states[0], (((1,), (1,)), ((), ())), preferred_element_type=jnp.float32
    ).astype(jnp.bfloat16)
    noisy_patch = (
        (1.0 - noise_level) * generated.astype(jnp.float32)
        + noise_level * noise_field[0].astype(jnp.float32)
    ).astype(jnp.bfloat16)
    sinus_wave = sinusoid(time_step)
    freq_rows = time_real.shape[0]
    own_wave = lax.dynamic_slice_in_dim(sinus_wave, lax.axis_index("tm") * freq_rows, freq_rows, 0)
    share_real = jnp.einsum("f,fcd->cd", own_wave, time_real, preferred_element_type=jnp.float32)
    share_fake = jnp.einsum("f,fcd->cd", own_wave, time_fake, preferred_element_type=jnp.float32)
    modul_real, modul_fake = lax.psum((share_real, share_fake), "tm")
    earlier = from_behind(noisy_patch, "tm", 1)
    stacked = jnp.concatenate([noisy_patch, earlier], axis=0)
    embedded_real, mean_real, rscale_real = embed_stats(stacked, embed_real)
    embedded_fake, mean_fake, rscale_fake = embed_stats(stacked, embed_fake)
    folded_real = fold_heads(embed_real, modul_real, query_real, key_real, value_real)
    folded_fake = fold_heads(embed_fake, modul_fake, query_fake, key_fake, value_fake)
    local_width = query_real.shape[1]
    local_heads = local_width // HD
    columns = local_width * devices
    gathered = (
        lax.all_gather(noisy_patch.astype(jnp.float32), "tm", axis=1, tiled=True),
        lax.all_gather(mean_real, "tm", axis=0, tiled=True),
        lax.all_gather(rscale_real, "tm", axis=0, tiled=True),
        lax.all_gather(mean_fake, "tm", axis=0, tiled=True),
        lax.all_gather(rscale_fake, "tm", axis=0, tiled=True),
    )
    all_patch = gathered[0].astype(jnp.bfloat16)
    prior_frame = jnp.concatenate(
        [
            jnp.zeros((patch_rows, frame_tokens), jnp.bfloat16),
            all_patch[:, : tokens - frame_tokens],
        ],
        axis=1,
    )
    all_stacked = jnp.concatenate([all_patch, prior_frame], axis=0)
    qkv_real = project(all_stacked, gathered[1], gathered[2], folded_real)
    qkv_fake = project(all_stacked, gathered[3], gathered[4], folded_fake)
    norm_sums = lax.psum(
        (
            jnp.sum(qkv_real[0] * qkv_real[0], axis=1),
            jnp.sum(qkv_real[1] * qkv_real[1], axis=1),
            jnp.sum(qkv_fake[0] * qkv_fake[0], axis=1),
            jnp.sum(qkv_fake[1] * qkv_fake[1], axis=1),
        ),
        "tm",
    )
    head_shape = (tokens, local_heads, HD)
    attended_real = attend(
        rms_round(qkv_real[0], norm_sums[0], columns, gain_real[0]).reshape(head_shape),
        rms_round(qkv_real[1], norm_sums[1], columns, gain_real[1]).reshape(head_shape),
        qkv_real[2].astype(jnp.bfloat16).reshape(head_shape),
    )
    attended_fake = attend(
        rms_round(qkv_fake[0], norm_sums[2], columns, gain_fake[0]).reshape(head_shape),
        rms_round(qkv_fake[1], norm_sums[3], columns, gain_fake[1]).reshape(head_shape),
        qkv_fake[2].astype(jnp.bfloat16).reshape(head_shape),
    )
    term_real = head_terms(attended_real, out_real, modul_real, proj_real)
    term_fake = head_terms(attended_fake, out_fake, modul_fake, proj_fake)
    own_real, own_fake = (
        lax.psum_scatter(term_real, "tm", scatter_dimension=1, tiled=True),
        lax.psum_scatter(term_fake, "tm", scatter_dimension=1, tiled=True),
    )
    velocity_real = own_real + lax.dot_general(
        proj_real.astype(jnp.float32), embedded_real, (((1,), (1,)), ((), ())), precision=highest
    )
    velocity_fake = own_fake + lax.dot_general(
        proj_fake.astype(jnp.float32), embedded_fake, (((1,), (1,)), ((), ())), precision=highest
    )
    pred_real = noisy_patch.astype(jnp.float32) - noise_level * velocity_real
    pred_fake = noisy_patch.astype(jnp.float32) - noise_level * velocity_fake
    gap_local = jnp.sum(jnp.abs(generated.astype(jnp.float32) - pred_real))
    count_all = patch_rows * tokens
    grad_root = math.sqrt(lax.axis_size("batch") * hidden_states.shape[0] * tokens)
    gap_diff = pred_fake - pred_real
    difference = gap_diff.astype(jnp.bfloat16)
    partial_grad = jnp.dot(difference, hidden_states[0], preferred_element_type=jnp.float32)
    gap_total = lax.psum(gap_local, "tm")
    normalizer = jnp.maximum(gap_total / count_all, gap_floor)
    weight_grad = lax.psum(partial_grad / normalizer / grad_root, ("tm", "batch"))
    dmd_gradient = (gap_diff / normalizer)[None]
    return (dmd_gradient, weight_grad)


def solution(mesh):
    in_specs = (
        P("batch", "tm", None),
        P(),
        P("batch", None, "tm"),
        P("batch"),
        P(),
        P("tm", None, None),
        P(None, "tm"),
        P(None, "tm"),
        P(None, "tm"),
        P("tm", None),
        P(None, "tm"),
        P(),
        P(),
        P("tm", None, None),
        P(None, "tm"),
        P(None, "tm"),
        P(None, "tm"),
        P("tm", None),
        P(None, "tm"),
        P(),
    )
    out_specs = (P("batch", None, "tm"), P())
    return jax.shard_map(
        per_device, mesh=mesh, in_specs=in_specs, out_specs=out_specs, check_vma=False
    )
```

profile of v0, /device:TPU:0, one launch (start us, length us, event | category | flops | bytes accessed | tf_op | source)
XLA Modules:
  0.0 419.4 jit_solution(4317178082355693844)
XLA Ops:
  8.5 2.4 fusion.74
  10.9 2.4 collective-permute-start
  16.0 25.7 %psum.59 = f32[3,5120]{1,0:T(4,128)S(1)} all-reduce(f32[3,5120]{1,0:T(4,128)S(1)} %bitcast.296), channel_id=1, replica_groups=mesh['tm'=8,'batch'=4] {'tm'}, use_global_device_ids=true, to_apply=%region_12.0 | all-reduce | flops 15360 | bytes 122880 | tf_op jit(solution)/shard_map/psum | solution.py:145
  54.8 3.7 fusion.20
  58.5 10.2 %all_gather.16 = bf16[64,1024]{1,0:T(8,128)(2,1)S(1)} all-gather(bf16[64,128]{1,0:T(8,128)(2,1)S(1)} %get-tuple-element.224), channel_id=1, replica_groups=mesh['tm'=8,'batch'=4] {'tm'}, dimensions={1}, use_global_device_ids=true | all-gather | bytes 147456 | tf_op jit(solution)/shard_map/all_gather | solution.py:156
  70.5 7.6 %all-gather.2 = f32[8,1,128]{2,1,0:T(1,128)S(1)} all-gather(f32[1,1,128]{2,1,0:T(1,128)S(1)} %rsqrt_bitcast_fusion), channel_id=1, replica_groups=mesh['tm'=8,'batch'=4] {'tm'}, dimensions={0}, use_global_device_ids=true | all-gather | bytes 4608 | tf_op jit(solution)/shard_map/all_gather | solution.py:158
  78.1 9.0 %all-gather.3 = f32[8,1,128]{2,1,0:T(1,128)S(1)} all-gather(f32[1,1,128]{2,1,0:T(1,128)S(1)} %get-tuple-element.222), channel_id=1, replica_groups=mesh['tm'=8,'batch'=4] {'tm'}, dimensions={0}, use_global_device_ids=true | all-gather | bytes 4608 | tf_op jit(solution)/shard_map/all_gather | solution.py:157
  94.5 7.9 %all-gather = f32[8,1,128]{2,1,0:T(1,128)S(1)} all-gather(f32[1,1,128]{2,1,0:T(1,128)} %rsqrt_bitcast_fusion.1), channel_id=1, replica_groups=mesh['tm'=8,'batch'=4] {'tm'}, dimensions={0}, use_global_device_ids=true | all-gather | bytes 4608 | tf_op jit(solution)/shard_map/all_gather | solution.py:160
  102.4 8.7 %all-gather.1 = f32[8,1,128]{2,1,0:T(1,128)S(1)} all-gather(f32[1,1,128]{2,1,0:T(1,128)} %get-tuple-element.220), channel_id=1, replica_groups=mesh['tm'=8,'batch'=4] {'tm'}, dimensions={0}, use_global_device_ids=true | all-gather | bytes 4608 | tf_op jit(solution)/shard_map/all_gather | solution.py:159
  111.7 33.1 %all-reduce.8.cloned.1.call-done = (f32[1024]{0:T(1024)}, f32[1024]{0:T(1024)}, f32[3,5120]{1,0:T(4,128)}) async-done(((f32[1024]{0:T(1024)}, f32[1024]{0:T(1024)}, f32[3,5120]{1,0:T(4,128)}), (f32[1024]{0:T(1024)}, f32[1024]{0:T(1024)}, f32[3,5120]{1,0:T(4,128)})) %all-reduce.8.cloned.1.call-update) | async-done | bytes 69648 | tf_op jit(solution)/shard_map/psum | solution.py:173
  146.5 2.0 fusion.93
  148.4 2.0 fusion.83
  158.9 9.1 %while.23 = (s32[]{:T(128)}, bf16[2,512,1,128]{3,1,2,0:T(8,128)(2,1)S(1)}, s32[1024]{0:T(1024)S(1)}, s32[2]{0:T(128)S(1)}, bf16[1024,1,128]{0,2,1:T(8,128)(2,1)S...) while((s32[]{:T(128)}, ...), condition=%wide.region_22.23_spmd.clone, body=%wide.region_19.22_spmd.clone.sunk | while | flops 273218560 | bytes 7098535 | solution.py:91
  169.4 2.1 fusion.30
  172.2 1.8 copy.41
  174.7 3.9 fusion.26
  178.6 25.1 %reduce-scatter.5.cloned.1.call-done = f32[64,128]{1,0:T(8,128)} async-done(((f32[64,1024]{1,0:T(8,128)}), f32[64,128]{1,0:T(8,128)}) %reduce-scatter.5.cloned.1.call-update) | async-done | bytes 32784 | tf_op jit(solution)/shard_map/reduce_scatter | solution.py:196
  203.6 4.6 %abs_reduce_fusion = (f32[]{:T(128)}, f32[64,128]{1,0:T(8,128)}) fusion(f32[64,128]{1,0:T(8,128)} %get-tuple-element.225, f32[64,128]{1,0:T(8,128)} %reduce-scatter.5.cloned.1.call-done, f32[128,5120]{1,0:T(8,128)} %copy-done.2, bf16[64,5120]{1,0:T(8,128)(2,1)S(1)} %copy-done.15, f32[]{:T(128)S(6)} %div.95, bf16[64,128]{1,0:T(8,128)(2,1)S(1)} %get-tuple-element.224), kind=kOutput, calls=%fused_computation.110 | convolution fusion | flops 503373824 | bytes 3391496 | tf_op jit(solution)/shard_map/dot_general | solution.py:199
  208.3 13.3 %all-reduce.1 = (f32[1024]{0:T(1024)S(1)}, f32[1024]{0:T(1024)S(1)}, f32[]{:T(128)}) all-reduce(f32[1024]{0:T(1024)} %get-tuple-element.163, f32[1024]{0:T(1024)} %get-tuple-element.162, f32[]{:T(128)} %get-tuple-element.230), channel_id=1, replica_groups=mesh['tm'=8,'batch'=4] {'tm'}, use_global_device_ids=true, to_apply=%region_4.0 | all-reduce | flops 2049 | bytes 16392 | tf_op jit(solution)/shard_map/psum | solution.py:173
  223.3 14.2 %while.22 = (s32[]{:T(128)}, bf16[2,512,1,128]{3,1,2,0:T(8,128)(2,1)S(1)}, s32[1024]{0:T(1024)}, s32[2]{0:T(128)}, bf16[1024,1,128]{0,2,1:T(8,128)(2,1)}, /*inde...) while((s32[]{:T(128)}, ...), condition=%wide.region_10.0_spmd.clone, body=%wide.region_7.10_spmd.clone.sunk | while | flops 273218560 | bytes 8147139 | solution.py:91
  239.3 33.3 %reduce-scatter.3.cloned.1.call-done = f32[64,128]{1,0:T(8,128)} async-done(((f32[64,1024]{1,0:T(8,128)}), f32[64,128]{1,0:T(8,128)}) %reduce-scatter.3.cloned.1.call-update) | async-done | bytes 32784 | tf_op jit(solution)/shard_map/reduce_scatter | solution.py:197
  272.6 3.4 fusion.46
  278.0 132.3 %all-reduce.6.cloned.1.call-done = f32[64,5120]{1,0:T(8,128)} async-done(((f32[64,5120]{1,0:T(8,128)}), f32[64,5120]{1,0:T(8,128)}) %all-reduce.6.cloned.1.call-update) | async-done | bytes 1310736 | tf_op jit(solution)/shard_map/psum | solution.py:215
  410.4 2.5 copy.87
  (176 shorter events, 59.2 us)
Async XLA Ops:
  7.2 137.6 %all-reduce.8.cloned.1.call-start = ((), (), s32[]{:S(2)}) async-start(), calls=%async_computation.5 | async-start | bytes 180224 | tf_op jit(solution)/shard_map/psum | solution.py:173
  8.5 33.3 %copy-start.5 = (bf16[5120,128]{1,0:T(8,128)(2,1)S(1)}, bf16[5120,128]{1,0:T(8,128)(2,1)}, u32[]{:S(2)}) copy-start(bf16[5120,128]{1,0:T(8,128)(2,1)} %param.32) | copy-start | bytes 3932164
  10.9 58.6 %collective-permute-start = (bf16[64,128]{1,0:T(8,128)(2,1)S(1)}, bf16[64,128]{1,0:T(8,128)(2,1)S(1)}, u32[]{:S(2)}, u32[]{:S(2)}) collective-permute-start(bf16[64,128]{1,0:T(8,128)(2,1)S(1)} %get-tuple-element.224), channel_id=1, source_target_pairs={{0,4},{4,8},{8,12},{12,16},{16,20},{20,24},{24,28},{1,5},{5,9},{9,... | collective-permute-start | bytes 49160 | tf_op jit(solution)/shard_map/ppermute | solution.py:18
  14.4 28.6 %copy-start.31 = (bf16[256]{0:T(256)(128)(2,1)}, bf16[256]{0:T(256)(128)(2,1)S(1)}, u32[]{:S(2)}) copy-start(bf16[256]{0:T(256)(128)(2,1)S(1)} %pad_maximum_fusion.9) | copy-start | bytes 1540
  50.6 3.6 copy-start.34
  50.6 4.2 %copy-start.15 = (bf16[64,5120]{1,0:T(8,128)(2,1)S(1)}, bf16[64,5120]{1,0:T(8,128)(2,1)}, u32[]{:S(2)}) copy-start(bf16[64,5120]{1,0:T(8,128)(2,1)} %param.35) | copy-start | bytes 1966084
  68.7 18.4 %copy-start.17 = (bf16[64,1024]{1,0:T(8,128)(2,1)}, bf16[64,1024]{1,0:T(8,128)(2,1)S(1)}, u32[]{:S(2)}) copy-start(bf16[64,1024]{1,0:T(8,128)(2,1)S(1)} %all_gather.16) | copy-start | bytes 393220
  68.7 18.4 %copy-start.25 = (bf16[64,896]{1,0:T(8,128)(2,1)}, bf16[64,896]{1,0:T(8,128)(2,1)S(1)}, u32[]{:S(2)}) copy-start(bf16[64,896]{1,0:T(8,128)(2,1)S(1)} %slice.122) | copy-start | bytes 344068
  70.1 18.1 %copy-start.2 = (f32[128,5120]{1,0:T(8,128)}, f32[128,5120]{1,0:T(8,128)S(1)}, u32[]{:S(2)}) copy-start(f32[128,5120]{1,0:T(8,128)S(1)} %get-tuple-element.227) | copy-start | bytes 7864324
  70.1 17.0 %copy-start.20 = (f32[3,130,128]{2,1,0:T(8,128)S(1)}, f32[3,130,128]{2,1,0:T(8,128)}, u32[]{:S(2)}) copy-start(f32[3,130,128]{2,1,0:T(8,128)} %pad_maximum_fusion.1) | copy-start | bytes 599044
  92.4 111.2 %reduce-scatter.5.cloned.1.call-start = ((), (), s32[]{:S(2)}) async-start(), calls=%async_computation.3 | async-start | bytes 294912 | tf_op jit(solution)/shard_map/reduce_scatter | solution.py:196
  102.4 42.3 %copy-start.28 = (f32[8,1,128]{2,1,0:T(1,128)}, f32[8,1,128]{2,1,0:T(1,128)S(1)}, u32[]{:S(2)}) copy-start(f32[8,1,128]{2,1,0:T(1,128)S(1)} %all-gather) | copy-start | bytes 12292
  144.8 5.7 %copy-start.10 = (bf16[5120,128]{1,0:T(8,128)(2,1)S(1)}, bf16[5120,128]{1,0:T(8,128)(2,1)}, u32[]{:S(2)}) copy-start(bf16[5120,128]{1,0:T(8,128)(2,1)} %param.39) | copy-start | bytes 3932164
  144.8 5.7 %copy-start.14 = (f32[3,5120]{1,0:T(4,128)S(1)}, f32[3,5120]{1,0:T(4,128)}, u32[]{:S(2)}) copy-start(f32[3,5120]{1,0:T(4,128)} %get-tuple-element.199) | copy-start | bytes 184324
  156.1 2.4 copy-start.29
  156.1 2.4 copy-start.13
  156.1 2.4 copy-start.32
  156.1 2.4 copy-start.33
  158.9 9.1 %copy-start.23 = (f32[128,64]{0,1:T(8,128)S(1)}, f32[128,64]{0,1:T(8,128)}, u32[]{:S(2)}) copy-start(f32[128,64]{0,1:T(8,128)} %fusion.20) | copy-start | bytes 98308
  169.1 103.5 %reduce-scatter.3.cloned.1.call-start = ((), (), s32[]{:S(2)}) async-start(), calls=%async_computation.2 | async-start | bytes 294912 | tf_op jit(solution)/shard_map/reduce_scatter | solution.py:197
  223.3 14.2 %copy-start.24 = (f32[128,64]{0,1:T(8,128)S(1)}, f32[128,64]{0,1:T(8,128)}, u32[]{:S(2)}) copy-start(f32[128,64]{0,1:T(8,128)} %fusion.26) | copy-start | bytes 98308
  223.3 49.3 %copy-start.16 = (bf16[64,5120]{1,0:T(8,128)(2,1)S(1)}, bf16[64,5120]{1,0:T(8,128)(2,1)}, u32[]{:S(2)}) copy-start(bf16[64,5120]{1,0:T(8,128)(2,1)} %param.43) | copy-start | bytes 1966084
  223.3 49.3 %copy-start.22 = (f32[64,128]{1,0:T(8,128)S(1)}, f32[64,128]{1,0:T(8,128)}, u32[]{:S(2)}) copy-start(f32[64,128]{1,0:T(8,128)} %get-tuple-element.231) | copy-start | bytes 98308
  238.6 171.7 %all-reduce.6.cloned.1.call-start = ((), (), s32[]{:S(2)}) async-start(), calls=%async_computation.4 | async-start | bytes 2621440 | tf_op jit(solution)/shard_map/psum | solution.py:215
  (18 other events, 25.7 us)
Sparse Core Ops, SparseCore 0:
  92.6 52.1 all-reduce.7
  169.2 34.3 reduce-scatter.4
  238.7 33.7 reduce-scatter.2
  278.4 131.9 all-reduce.5
where the time goes:
time: 421 us; the launch traced here: 419 us
  waiting for transfers between devices  224 us (53%)
  blocking collectives  82.3 us (20%)
  matrix products  55.5 us (13%)
  local copies, waits for them, and re-layouts  17.6 us (4%)
  between operations  15.8 us (4%)
  other arithmetic  13.9 us (3%)
  loops' own time  7.68 us (2%)
    psum x1, waiting for transfers between devices, per_device(): lax.psum(partial_grad / normalizer / grad_root, ('tm', 'batch'))  132 us
    reduce_scatter x1, waiting for transfers between devices, per_device(): lax.psum_scatter(term_fake, 'tm', scatter_dimension=1, tiled=True)  33.3 us
    psum x1, waiting for transfers between devices, per_device(): lax.psum((jnp.sum(qkv_real[0] * qkv_real[0], axis=1), jnp.sum(qkv_real[1]...  33.1 us
    psum x1, blocking collectives, per_device(): modul_real, modul_fake = lax.psum((share_real, share_fake), 'tm')  25.7 us
    reduce_scatter x1, waiting for transfers between devices, per_device(): lax.psum_scatter(term_real, 'tm', scatter_dimension=1, tiled=True)  25.1 us
    psum x1, blocking collectives, per_device(): lax.psum((jnp.sum(qkv_real[0] * qkv_real[0], axis=1), jnp.sum(qkv_real[1]...  13.3 us
    all_gather x1, blocking collectives, per_device(): lax.all_gather(noisy_patch.astype(jnp.float32), 'tm', axis=1, tiled=True)  10.2 us
    dot_general x6, matrix products, fold_one(): main_part = jnp.dot(widened, wide_weight, precision=highest)  9.04 us
  transfers between devices with their start and end apart: 5, of which 4 were waited for; matrix products, arithmetic and copies ran while one was open for 8% of the time, Pallas kernels for 0%

commit v1 on v0

--- a/solution.py
+++ b/solution.py
@@ -212,7 +212,9 @@
     partial_grad = jnp.dot(difference, hidden_states[0], preferred_element_type=jnp.float32)
     gap_total = lax.psum(gap_local, "tm")
     normalizer = jnp.maximum(gap_total / count_all, gap_floor)
-    weight_grad = lax.psum(partial_grad / normalizer / grad_root, ("tm", "batch"))
+    weight_grad = jnp.sum(
+        lax.all_gather(partial_grad / normalizer / grad_root, ("tm", "batch")), axis=0
+    )
     dmd_gradient = (gap_diff / normalizer)[None]
     return (dmd_gradient, weight_grad)
 

time: 421 us -> 531 us (1.26)
  waiting for transfers between devices: 224 us -> 325 us
  other arithmetic: 13.9 us -> 27.9 us
  local copies, waits for them, and re-layouts: 17.6 us -> 12 us
    all_gather x0 -> x1, waiting for transfers between devices: none -> 234 us  [per_device(): lax.all_gather(partial_grad / normalizer / grad_root, ('tm', 'batch'))]
    psum x1 -> x0, waiting for transfers between devices: 132 us -> none  [per_device(): lax.psum(partial_grad / normalizer / grad_root, ('tm', 'batch'))]
    reduce_sum x0 -> x1, other arithmetic: none -> 15.7 us  [per_device(): jnp.sum(lax.all_gather(partial_grad / normalizer / grad_root, ('tm', 'bat...]
  transfers between devices with their start and end apart: 5 -> 5, of which waited for: 4 -> 4; matrix products, arithmetic and copies ran while one was open for 8% -> 6% of each run, Pallas kernels for 0% -> 0%
where the time goes in v1:
time: 531 us; the launch traced here: 530 us
  waiting for transfers between devices  325 us (61%)
  blocking collectives  81.9 us (15%)
  matrix products  55.9 us (11%)
  other arithmetic  27.9 us (5%)
  between operations  15.8 us (3%)
  local copies, waits for them, and re-layouts  12 us (2%)
  loops' own time  7.32 us (1%)
    all_gather x1, waiting for transfers between devices, per_device(): lax.all_gather(partial_grad / normalizer / grad_root, ('tm', 'batch'))  234 us
    reduce_scatter x1, waiting for transfers between devices, per_device(): lax.psum_scatter(term_fake, 'tm', scatter_dimension=1, tiled=True)  33.2 us
    psum x1, waiting for transfers between devices, per_device(): lax.psum((jnp.sum(qkv_real[0] * qkv_real[0], axis=1), jnp.sum(qkv_real[1]...  33.1 us
    psum x1, blocking collectives, per_device(): modul_real, modul_fake = lax.psum((share_real, share_fake), 'tm')  25.3 us
    reduce_scatter x1, waiting for transfers between devices, per_device(): lax.psum_scatter(term_real, 'tm', scatter_dimension=1, tiled=True)  25.1 us
    reduce_sum x1, other arithmetic, per_device(): jnp.sum(lax.all_gather(partial_grad / normalizer / grad_root, ('tm', 'bat...  15.7 us
    psum x1, blocking collectives, per_device(): lax.psum((jnp.sum(qkv_real[0] * qkv_real[0], axis=1), jnp.sum(qkv_real[1]...  13.3 us
  transfers between devices with their start and end apart: 5, of which 4 were waited for; matrix products, arithmetic and copies ran while one was open for 6% of the time, Pallas kernels for 0%

profile of v1, /device:TPU:0, one launch (start us, length us, event | category | flops | bytes accessed | tf_op | source)
XLA Modules:
  0.0 529.6 jit_solution(6165187895158613940)
XLA Ops:
  8.5 2.3 fusion.74
  10.8 3.0 collective-permute-start
  15.8 25.3 %psum.52 = f32[3,5120]{1,0:T(4,128)S(1)} all-reduce(f32[3,5120]{1,0:T(4,128)S(1)} %bitcast.298), channel_id=1, replica_groups=mesh['tm'=8,'batch'=4] {'tm'}, use_global_device_ids=true, to_apply=%region_12.0 | all-reduce | flops 15360 | bytes 122880 | tf_op jit(solution)/shard_map/psum | solution.py:145
  43.0 1.9 fusion.97
  54.4 2.4 fusion.20
  56.8 10.2 %all_gather.22 = bf16[64,1024]{1,0:T(8,128)(2,1)S(1)} all-gather(bf16[64,128]{1,0:T(8,128)(2,1)S(1)} %get-tuple-element.224), channel_id=1, replica_groups=mesh['tm'=8,'batch'=4] {'tm'}, dimensions={1}, use_global_device_ids=true | all-gather | bytes 147456 | tf_op jit(solution)/shard_map/all_gather | solution.py:156
  68.8 7.6 %all-gather.3 = f32[8,1,128]{2,1,0:T(1,128)S(1)} all-gather(f32[1,1,128]{2,1,0:T(1,128)S(1)} %rsqrt_bitcast_fusion), channel_id=1, replica_groups=mesh['tm'=8,'batch'=4] {'tm'}, dimensions={0}, use_global_device_ids=true | all-gather | bytes 4608 | tf_op jit(solution)/shard_map/all_gather | solution.py:158
  76.5 9.0 %all-gather.4 = f32[8,1,128]{2,1,0:T(1,128)S(1)} all-gather(f32[1,1,128]{2,1,0:T(1,128)S(1)} %get-tuple-element.222), channel_id=1, replica_groups=mesh['tm'=8,'batch'=4] {'tm'}, dimensions={0}, use_global_device_ids=true | all-gather | bytes 4608 | tf_op jit(solution)/shard_map/all_gather | solution.py:157
  93.5 7.9 %all-gather.1 = f32[8,1,128]{2,1,0:T(1,128)S(1)} all-gather(f32[1,1,128]{2,1,0:T(1,128)} %rsqrt_bitcast_fusion.1), channel_id=1, replica_groups=mesh['tm'=8,'batch'=4] {'tm'}, dimensions={0}, use_global_device_ids=true | all-gather | bytes 4608 | tf_op jit(solution)/shard_map/all_gather | solution.py:160
  101.4 8.7 %all-gather.2 = f32[8,1,128]{2,1,0:T(1,128)S(1)} all-gather(f32[1,1,128]{2,1,0:T(1,128)} %get-tuple-element.220), channel_id=1, replica_groups=mesh['tm'=8,'batch'=4] {'tm'}, dimensions={0}, use_global_device_ids=true | all-gather | bytes 4608 | tf_op jit(solution)/shard_map/all_gather | solution.py:159
  110.7 33.1 %all-reduce.5.cloned.1.call-done = (f32[1024]{0:T(1024)}, f32[1024]{0:T(1024)}, f32[3,5120]{1,0:T(4,128)}) async-done(((f32[1024]{0:T(1024)}, f32[1024]{0:T(1024)}, f32[3,5120]{1,0:T(4,128)}), (f32[1024]{0:T(1024)}, f32[1024]{0:T(1024)}, f32[3,5120]{1,0:T(4,128)})) %all-reduce.5.cloned.1.call-update) | async-done | bytes 69648 | tf_op jit(solution)/shard_map/psum | solution.py:173
  143.8 2.1 fusion.85
  145.9 2.0 fusion.94
  158.2 9.1 %while.23 = (s32[]{:T(128)}, bf16[2,512,1,128]{3,1,2,0:T(8,128)(2,1)S(1)}, s32[1024]{0:T(1024)S(1)}, s32[2]{0:T(128)S(1)}, bf16[1024,1,128]{0,2,1:T(8,128)(2,1)S...) while((s32[]{:T(128)}, ...), condition=%wide.region_22.23_spmd.clone, body=%wide.region_19.22_spmd.clone.sunk | while | flops 273218560 | bytes 7098535 | solution.py:91
  168.6 2.1 fusion.30
  173.9 3.9 fusion.26
  177.8 25.1 %reduce-scatter.5.cloned.1.call-done = f32[64,128]{1,0:T(8,128)} async-done(((f32[64,1024]{1,0:T(8,128)}), f32[64,128]{1,0:T(8,128)}) %reduce-scatter.5.cloned.1.call-update) | async-done | bytes 32784 | tf_op jit(solution)/shard_map/reduce_scatter | solution.py:196
  202.9 4.6 abs_reduce_fusion
  207.5 13.3 %all-reduce.1 = (f32[1024]{0:T(1024)S(1)}, f32[1024]{0:T(1024)S(1)}, f32[]{:T(128)}) all-reduce(f32[1024]{0:T(1024)} %get-tuple-element.163, f32[1024]{0:T(1024)} %get-tuple-element.162, f32[]{:T(128)} %get-tuple-element.230), channel_id=1, replica_groups=mesh['tm'=8,'batch'=4] {'tm'}, use_global_device_ids=true, to_apply=%region_4.0 | all-reduce | flops 2049 | bytes 16392 | tf_op jit(solution)/shard_map/psum | solution.py:173
  222.6 10.4 %while.22 = (s32[]{:T(128)}, bf16[2,512,1,128]{3,1,2,0:T(8,128)(2,1)S(1)}, s32[1024]{0:T(1024)S(1)}, s32[2]{0:T(128)S(1)}, bf16[1024,1,128]{0,2,1:T(8,128)(2,1)}...) while((s32[]{:T(128)}, ...), condition=%wide.region_10.0_spmd.clone, body=%wide.region_7.10_spmd.clone.sunk | while | flops 273218560 | bytes 7098535 | solution.py:91
  234.8 33.2 %reduce-scatter.3.cloned.1.call-done = f32[64,128]{1,0:T(8,128)} async-done(((f32[64,1024]{1,0:T(8,128)}), f32[64,128]{1,0:T(8,128)}) %reduce-scatter.3.cloned.1.call-update) | async-done | bytes 32784 | tf_op jit(solution)/shard_map/reduce_scatter | solution.py:197
  268.0 3.4 fusion.46
  273.4 234.0 %all-gather.7.cloned.1.call-done = f32[2048,5120]{1,0:T(8,128)} async-done(((f32[64,5120]{1,0:T(8,128)}), f32[2048,5120]{1,0:T(8,128)}) %all-gather.7.cloned.1.call-update) | async-done | bytes 41943056 | tf_op jit(solution)/shard_map/all_gather | solution.py:216
  507.4 15.7 %reduce_sum.117 = f32[64,5120]{1,0:T(8,128)} reduce(f32[32,64,5120]{2,1,0:T(8,128)} %bitcast.288, f32[]{:T(128)} %constant.103.clone.1), dimensions={0}, to_apply=%region_26.27 | reduce | flops 10158080 | bytes 43253764 | tf_op jit(solution)/shard_map/reduce_sum | solution.py:215
  (180 shorter events, 55.9 us)
Async XLA Ops:
  7.2 8.3 %copy-start.17 = (bf16[32,3,5120]{2,0,1:T(8,128)(2,1)S(1)}, bf16[32,3,5120]{2,0,1:T(8,128)(2,1)}, u32[]{:S(2)}) copy-start(bf16[32,3,5120]{2,0,1:T(8,128)(2,1)} %param.29) | copy-start | bytes 2949124
  7.2 136.6 %all-reduce.5.cloned.1.call-start = ((), (), s32[]{:S(2)}) async-start(), calls=%async_computation.5 | async-start | bytes 180224 | tf_op jit(solution)/shard_map/psum | solution.py:173
  10.8 56.3 %collective-permute-start = (bf16[64,128]{1,0:T(8,128)(2,1)S(1)}, bf16[64,128]{1,0:T(8,128)(2,1)}, u32[]{:S(2)}, u32[]{:S(2)}) collective-permute-start(bf16[64,128]{1,0:T(8,128)(2,1)S(1)} %get-tuple-element.224), channel_id=1, source_target_pairs={{0,4},{4,8},{8,12},{12,16},{16,20},{20,24},{24,28},{1,5},{5,9},{9,... | collective-permute-start | bytes 49160 | tf_op jit(solution)/shard_map/ppermute | solution.py:18
  15.8 29.2 %copy-start.5 = (bf16[5120,128]{1,0:T(8,128)(2,1)S(1)}, bf16[5120,128]{1,0:T(8,128)(2,1)}, u32[]{:S(2)}) copy-start(bf16[5120,128]{1,0:T(8,128)(2,1)} %param.32) | copy-start | bytes 3932164
  50.6 2.8 copy-start.18
  67.0 18.4 %copy-start.19 = (bf16[64,1024]{1,0:T(8,128)(2,1)}, bf16[64,1024]{1,0:T(8,128)(2,1)S(1)}, u32[]{:S(2)}) copy-start(bf16[64,1024]{1,0:T(8,128)(2,1)S(1)} %all_gather.22) | copy-start | bytes 393220
  67.0 18.4 %copy-start.27 = (bf16[64,896]{1,0:T(8,128)(2,1)}, bf16[64,896]{1,0:T(8,128)(2,1)S(1)}, u32[]{:S(2)}) copy-start(bf16[64,896]{1,0:T(8,128)(2,1)S(1)} %slice.122) | copy-start | bytes 344068
  68.4 18.0 %copy-start.2 = (f32[128,5120]{1,0:T(8,128)}, f32[128,5120]{1,0:T(8,128)S(1)}, u32[]{:S(2)}) copy-start(f32[128,5120]{1,0:T(8,128)S(1)} %get-tuple-element.227) | copy-start | bytes 7864324
  91.4 111.4 %reduce-scatter.5.cloned.1.call-start = ((), (), s32[]{:S(2)}) async-start(), calls=%async_computation.3 | async-start | bytes 294912 | tf_op jit(solution)/shard_map/reduce_scatter | solution.py:196
  101.4 47.1 %copy-start.28 = (f32[8,1,128]{2,1,0:T(1,128)}, f32[8,1,128]{2,1,0:T(1,128)S(1)}, u32[]{:S(2)}) copy-start(f32[8,1,128]{2,1,0:T(1,128)S(1)} %all-gather.1) | copy-start | bytes 12292
  143.8 4.1 copy-start.8
  143.8 4.1 copy-start.13
  154.2 3.6 copy-start.12
  154.2 3.5 copy-start.33
  154.2 3.5 copy-start.34
  158.1 9.1 %copy-start.25 = (f32[128,64]{0,1:T(8,128)S(1)}, f32[128,64]{0,1:T(8,128)}, u32[]{:S(2)}) copy-start(f32[128,64]{0,1:T(8,128)} %fusion.20) | copy-start | bytes 98308
  168.3 99.6 %reduce-scatter.3.cloned.1.call-start = ((), (), s32[]{:S(2)}) async-start(), calls=%async_computation.2 | async-start | bytes 294912 | tf_op jit(solution)/shard_map/reduce_scatter | solution.py:197
  207.5 15.0 %copy-start.21 = (bf16[1024,1,128]{2,0,1:T(8,128)(2,1)S(1)}, bf16[1024,1,128]{2,0,1:T(8,128)(2,1)}, u32[]{:S(2)}) copy-start(bf16[1024,1,128]{2,0,1:T(8,128)(2,1)} %copy.41) | copy-start | bytes 786436
  207.5 15.0 %copy-start.23 = (s32[1024]{0:T(1024)S(1)}, s32[1024]{0:T(1024)}, u32[]{:S(2)}) copy-start(s32[1024]{0:T(1024)} %add_select_fusion) | copy-start | bytes 12292
  207.5 15.0 %copy-start.38 = (s32[2]{0:T(128)S(1)}, s32[2]{0:T(128)}, u32[]{:S(2)}) copy-start(s32[2]{0:T(128)} %iota_multiply_fusion) | copy-start | bytes 28
  222.6 10.4 %copy-start.26 = (f32[128,64]{0,1:T(8,128)S(1)}, f32[128,64]{0,1:T(8,128)}, u32[]{:S(2)}) copy-start(f32[128,64]{0,1:T(8,128)} %fusion.26) | copy-start | bytes 98308
  222.6 45.4 %copy-start.15 = (bf16[64,5120]{1,0:T(8,128)(2,1)S(1)}, bf16[64,5120]{1,0:T(8,128)(2,1)}, u32[]{:S(2)}) copy-start(bf16[64,5120]{1,0:T(8,128)(2,1)} %param.43) | copy-start | bytes 1966084
  222.6 45.4 %copy-start.24 = (f32[64,128]{1,0:T(8,128)S(1)}, f32[64,128]{1,0:T(8,128)}, u32[]{:S(2)}) copy-start(f32[64,128]{1,0:T(8,128)} %get-tuple-element.231) | copy-start | bytes 98308
  234.1 273.3 %all-gather.7.cloned.1.call-start = ((), (), s32[]{:S(2)}) async-start(), calls=%async_computation.4 | async-start | bytes 43253760 | tf_op jit(solution)/shard_map/all_gather | solution.py:216
  (20 other events, 37.4 us)
Sparse Core Ops, SparseCore 0:
  91.6 52.2 all-reduce.4
  168.5 34.3 reduce-scatter.4
  234.2 33.6 reduce-scatter.2
  272.9 234.4 all-gather.6
